TPU v7x, 32 devices: a whole 2x2x4 slice. The times are simulated.
32 devices in a mesh: row: 8 (over z, core), col: 4 (over y, x).
Axes of the slice: x: 2, y: 2, z: 4, core: 2. Of those that a mesh axis runs over, the one named last changes fastest.
Arguments:
- right_sides: float32 [4, 1024, 4096], P(None, 'row', 'col'), may hold values from -6 to 6
- low_left: bfloat16 [6, 4096, 128], P(None, 'col'), may hold values from -0.25 to 0.25
- low_right: bfloat16 [6, 4096, 128], P(None, 'col'), may hold values from -0.09375 to 0.09375
- up_left: bfloat16 [6, 4096, 128], P(None, 'col'), may hold values from -0.25 to 0.25
- up_right: bfloat16 [6, 4096, 128], P(None, 'col'), may hold values from -0.09375 to 0.09375
- low_ranks: int32 [6], replicated, may hold values from 1 to 4
- up_ranks: int32 [6], replicated, may hold values from 1 to 4
- inv_lower: bfloat16 [4, 4096, 4096], P(None, 'col', 'row'), may hold values from -0.09375 to 0.09375
- inv_upper: bfloat16 [4, 4096, 4096], P(None, 'col', 'row'), may hold values from -0.09375 to 0.09375
Outputs:
- solution: float32 [4, 1024, 4096], P(None, 'row', 'col')
Inputs may be any that keep to these rules, and one draw needn't show every extreme that they name: `low_ranks`: factor columns beyond 32 times this value are padding with arbitrary values and must be masked out. `up_ranks`: factor columns beyond 32 times this value are padding with arbitrary values and must be masked out.
All inputs are finite; a program needn't handle non-finite values.
Results may differ from a plain program's by a relative error of at most 0.03.
Values may be sent and summed in bfloat16 or wider, within the bound.
A program may use at most 64 MiB of HBM per device.

v0:
```python
import jax
import jax.numpy as jnp
import numpy as np
from jax import lax
from jax.sharding import PartitionSpec as P

RBLK = 32


def rank_mask(ranks, pair_index, rank_cols):
    columns = jnp.arange(rank_cols, dtype=jnp.int32)
    return (columns[None, :] < RBLK * ranks[pair_index][:, None]).astype(jnp.float32)


def times_inverse(block, inverse):
    return lax.dot_general(
        block, inverse, (((1,), (1,)), ((), ())), preferred_element_type=jnp.float32
    )


def sum_terms(moved, inverse):
    return times_inverse(moved, inverse)


def shards(
    right_sides, low_left, low_right, up_left, up_right, low_ranks, up_ranks, inv_lower, inv_upper
):
    tile_count = right_sides.shape[0]
    rank_cols = low_left.shape[2]
    residual = right_sides
    forward = []
    for section in range(tile_count):
        rounded = residual[section].astype(jnp.bfloat16)
        whole = lax.all_gather(rounded, "col", axis=1, tiled=True)
        moved = lax.all_to_all(whole, "row", split_axis=1, concat_axis=0, tiled=True)
        solved = lax.psum_scatter(
            sum_terms(moved, inv_lower[section]).astype(jnp.bfloat16),
            "row",
            scatter_dimension=0,
            tiled=True,
        ).astype(jnp.float32)
        forward.append(solved)
        if section + 1 < tile_count:
            pair_index = np.array(
                [tile * (tile - 1) // 2 + section for tile in range(section + 1, tile_count)],
                dtype=np.int32,
            )
            projections = jnp.einsum(
                "nw,mwr->mnr",
                solved.astype(jnp.bfloat16),
                low_right[pair_index],
                preferred_element_type=jnp.float32,
            )
            leading = lax.psum(projections[:1].astype(jnp.bfloat16), "col").astype(jnp.float32)
            if section + 2 < tile_count:
                remaining = lax.psum(projections[1:].astype(jnp.bfloat16), "col").astype(
                    jnp.float32
                )
                summed = jnp.concatenate([leading, remaining], axis=0)
            else:
                summed = leading
            masked = (summed * rank_mask(low_ranks, pair_index, rank_cols)[:, None, :]).astype(
                jnp.bfloat16
            )
            update = jnp.einsum(
                "mnr,mwr->mnw", masked, low_left[pair_index], preferred_element_type=jnp.float32
            )
            residual = residual.at[section + 1 :].add(-update)
    state = jnp.stack(forward)
    solutions = [None] * tile_count
    for section in range(tile_count - 1, -1, -1):
        rounded = state[section].astype(jnp.bfloat16)
        whole = lax.all_gather(rounded, "col", axis=1, tiled=True)
        moved = lax.all_to_all(whole, "row", split_axis=1, concat_axis=0, tiled=True)
        solved = lax.psum_scatter(
            sum_terms(moved, inv_upper[section]).astype(jnp.bfloat16),
            "row",
            scatter_dimension=0,
            tiled=True,
        ).astype(jnp.float32)
        solutions[section] = solved
        if section > 0:
            pair_index = np.array(
                [section * (section - 1) // 2 + tile for tile in range(section)], dtype=np.int32
            )
            projections = jnp.einsum(
                "nw,mwr->mnr",
                solved.astype(jnp.bfloat16),
                up_right[pair_index],
                preferred_element_type=jnp.float32,
            )
            leading = lax.psum(projections[-1:].astype(jnp.bfloat16), "col").astype(jnp.float32)
            if section > 1:
                remaining = lax.psum(projections[:-1].astype(jnp.bfloat16), "col").astype(
                    jnp.float32
                )
                summed = jnp.concatenate([remaining, leading], axis=0)
            else:
                summed = leading
            masked = (summed * rank_mask(up_ranks, pair_index, rank_cols)[:, None, :]).astype(
                jnp.bfloat16
            )
            update = jnp.einsum(
                "mnr,mwr->mnw", masked, up_left[pair_index], preferred_element_type=jnp.float32
            )
            state = state.at[:section].add(-update)
    return jnp.stack(solutions)


def solution(mesh):
    in_specs = (
        P(None, "row", "col"),
        P(None, "col", None),
        P(None, "col", None),
        P(None, "col", None),
        P(None, "col", None),
        P(),
        P(),
        P(None, "col", "row"),
        P(None, "col", "row"),
    )
    out_specs = P(None, "row", "col")
    return jax.shard_map(shards, mesh=mesh, in_specs=in_specs, out_specs=out_specs, check_vma=False)
```

profile of v0, /device:TPU:0, one launch (start us, length us, event | category | flops | bytes accessed | tf_op | source)
XLA Modules:
  0.0 1013.5 jit_solution(5519528377490401830)
XLA Ops:
  8.5 29.9 %all-gather.18.cloned.1.call-done = bf16[1,128,4096]{1,2,0:T(8,128)(2,1)} async-done(((bf16[1,128,1024]{1,2,0:T(8,128)(2,1)}), bf16[1,128,4096]{1,2,0:T(8,128)(2,1)}) %all-gather.18.cloned.1.call-update) | async-done | bytes 1048592 | tf_op jit(solution)/shard_map/all_gather | solution.py:34
  38.4 31.2 %all_to_all.152 = bf16[128,8,512]{0,2,1:T(8,128)(2,1)S(1)} all-to-all(bf16[128,8,512]{0,2,1:T(8,128)(2,1)} %bitcast.171), channel_id=1, replica_groups=mesh['row'=8,'col'=4] {'row'}, dimensions={1} | all-to-all | bytes 2097152 | tf_op jit(solution)/shard_map/all_to_all | solution.py:35
  76.8 31.4 %reduce-scatter.9.cloned.1.call-done = bf16[128,1024]{1,0:T(8,128)(2,1)} async-done(((bf16[1024,1024]{1,0:T(8,128)(2,1)}), bf16[128,1024]{1,0:T(8,128)(2,1)}) %reduce-scatter.9.cloned.1.call-update) | async-done | bytes 262160 | tf_op jit(solution)/shard_map/reduce_scatter | solution.py:36
  154.2 26.6 %all-gather.20.cloned.1.call-done = bf16[1,128,4096]{2,1,0:T(8,128)(2,1)} async-done(((bf16[1,128,1024]{2,1,0:T(8,128)(2,1)}), bf16[1,128,4096]{2,1,0:T(8,128)(2,1)}) %all-gather.20.cloned.1.call-update) | async-done | bytes 1048592 | tf_op jit(solution)/shard_map/all_gather | solution.py:34
  182.8 31.0 %all_to_all.153 = bf16[128,8,512]{2,0,1:T(8,128)(2,1)S(1)} all-to-all(bf16[128,8,512]{2,0,1:T(8,128)(2,1)S(1)} %copy.61), channel_id=1, replica_groups=mesh['row'=8,'col'=4] {'row'}, dimensions={1} | all-to-all | bytes 2097152 | tf_op jit(solution)/shard_map/all_to_all | solution.py:35
  220.9 30.8 %reduce-scatter.11.cloned.1.call-done = bf16[128,1024]{1,0:T(8,128)(2,1)} async-done(((bf16[1024,1024]{1,0:T(8,128)(2,1)}), bf16[128,1024]{1,0:T(8,128)(2,1)}) %reduce-scatter.11.cloned.1.call-update) | async-done | bytes 262160 | tf_op jit(solution)/shard_map/reduce_scatter | solution.py:36
  255.9 39.0 %all-reduce.13.cloned.1.call-done = (bf16[1,128,128]{1,2,0:T(8,128)(2,1)}, bf16[1,128,128]{1,2,0:T(8,128)(2,1)}) async-done(((bf16[1,128,128]{1,2,0:T(8,128)(2,1)}, bf16[1,128,128]{1,2,0:T(8,128)(2,1)}), (bf16[1,128,128]{1,2,0:T(8,128)(2,1)}, bf16[1,128,128]{1,2,0:T(8,128)(2,1)})) %all-reduce.13.cloned.1.call-update) | async-done | bytes 65552 | tf_op jit(solution)/shard_map/psum | solution.py:56
  297.0 26.6 %all-gather.22.cloned.1.call-done = bf16[1,128,4096]{2,1,0:T(8,128)(2,1)} async-done(((bf16[1,128,1024]{2,1,0:T(8,128)(2,1)}), bf16[1,128,4096]{2,1,0:T(8,128)(2,1)}) %all-gather.22.cloned.1.call-update) | async-done | bytes 1048592 | tf_op jit(solution)/shard_map/all_gather | solution.py:34
  325.5 31.0 %all_to_all.154 = bf16[128,8,512]{2,0,1:T(8,128)(2,1)S(1)} all-to-all(bf16[128,8,512]{2,0,1:T(8,128)(2,1)S(1)} %copy.64), channel_id=1, replica_groups=mesh['row'=8,'col'=4] {'row'}, dimensions={1} | all-to-all | bytes 2097152 | tf_op jit(solution)/shard_map/all_to_all | solution.py:35
  361.6 32.9 %reduce-scatter.13.cloned.1.call-done = bf16[128,1024]{1,0:T(8,128)(2,1)} async-done(((bf16[1024,1024]{1,0:T(8,128)(2,1)}), bf16[128,1024]{1,0:T(8,128)(2,1)}) %reduce-scatter.13.cloned.1.call-update) | async-done | bytes 262160 | tf_op jit(solution)/shard_map/reduce_scatter | solution.py:36
  438.9 31.0 %all_to_all.155 = bf16[128,8,512]{2,0,1:T(8,128)(2,1)S(1)} all-to-all(bf16[128,8,512]{2,0,1:T(8,128)(2,1)S(1)} %copy.65), channel_id=1, replica_groups=mesh['row'=8,'col'=4] {'row'}, dimensions={1} | all-to-all | bytes 2097152 | tf_op jit(solution)/shard_map/all_to_all | solution.py:35
  473.8 34.1 %reduce-scatter.15.cloned.1.call-done = bf16[128,1024]{1,0:T(8,128)(2,1)} async-done(((bf16[1024,1024]{1,0:T(8,128)(2,1)}), bf16[128,1024]{1,0:T(8,128)(2,1)}) %reduce-scatter.15.cloned.1.call-update) | async-done | bytes 262160 | tf_op jit(solution)/shard_map/reduce_scatter | solution.py:36
  508.0 26.8 %all-gather.16.cloned.1.call-done = bf16[128,4096]{1,0:T(8,128)(2,1)} async-done(((bf16[128,1024]{1,0:T(8,128)(2,1)}), bf16[128,4096]{1,0:T(8,128)(2,1)}) %all-gather.16.cloned.1.call-update) | async-done | bytes 1048592 | tf_op jit(solution)/shard_map/all_gather | solution.py:73
  536.1 31.0 %all_to_all.156 = bf16[128,8,512]{2,0,1:T(8,128)(2,1)S(1)} all-to-all(bf16[128,8,512]{2,0,1:T(8,128)(2,1)S(1)} %bitcast.165), channel_id=1, replica_groups=mesh['row'=8,'col'=4] {'row'}, dimensions={1} | all-to-all | bytes 2097152 | tf_op jit(solution)/shard_map/all_to_all | solution.py:74
  573.8 31.4 %reduce-scatter.17.cloned.1.call-done = bf16[128,1024]{1,0:T(8,128)(2,1)} async-done(((bf16[1024,1024]{1,0:T(8,128)(2,1)}), bf16[128,1024]{1,0:T(8,128)(2,1)}) %reduce-scatter.17.cloned.1.call-update) | async-done | bytes 262160 | tf_op jit(solution)/shard_map/reduce_scatter | solution.py:75
  650.6 26.6 %all-gather.26.cloned.1.call-done = bf16[1,128,4096]{2,1,0:T(8,128)(2,1)} async-done(((bf16[1,128,1024]{2,1,0:T(8,128)(2,1)}), bf16[1,128,4096]{2,1,0:T(8,128)(2,1)}) %all-gather.26.cloned.1.call-update) | async-done | bytes 1048592 | tf_op jit(solution)/shard_map/all_gather | solution.py:73
  679.1 31.0 %all_to_all.157 = bf16[128,8,512]{2,0,1:T(8,128)(2,1)S(1)} all-to-all(bf16[128,8,512]{2,0,1:T(8,128)(2,1)S(1)} %copy.69), channel_id=1, replica_groups=mesh['row'=8,'col'=4] {'row'}, dimensions={1} | all-to-all | bytes 2097152 | tf_op jit(solution)/shard_map/all_to_all | solution.py:74
  717.3 30.9 %reduce-scatter.19.cloned.1.call-done = bf16[128,1024]{1,0:T(8,128)(2,1)} async-done(((bf16[1024,1024]{1,0:T(8,128)(2,1)}), bf16[128,1024]{1,0:T(8,128)(2,1)}) %reduce-scatter.19.cloned.1.call-update) | async-done | bytes 262160 | tf_op jit(solution)/shard_map/reduce_scatter | solution.py:75
  752.3 39.0 %all-reduce.11.cloned.1.call-done = (bf16[1,128,128]{1,2,0:T(8,128)(2,1)}, bf16[1,128,128]{1,2,0:T(8,128)(2,1)}) async-done(((bf16[1,128,128]{1,2,0:T(8,128)(2,1)}, bf16[1,128,128]{1,2,0:T(8,128)(2,1)}), (bf16[1,128,128]{1,2,0:T(8,128)(2,1)}, bf16[1,128,128]{1,2,0:T(8,128)(2,1)})) %all-reduce.11.cloned.1.call-update) | async-done | bytes 65552 | tf_op jit(solution)/shard_map/psum | solution.py:92
  793.3 26.6 %all-gather.28.cloned.1.call-done = bf16[1,128,4096]{2,1,0:T(8,128)(2,1)} async-done(((bf16[1,128,1024]{2,1,0:T(8,128)(2,1)}), bf16[1,128,4096]{2,1,0:T(8,128)(2,1)}) %all-gather.28.cloned.1.call-update) | async-done | bytes 1048592 | tf_op jit(solution)/shard_map/all_gather | solution.py:73
  821.8 31.0 %all_to_all.158 = bf16[128,8,512]{2,0,1:T(8,128)(2,1)S(1)} all-to-all(bf16[128,8,512]{2,0,1:T(8,128)(2,1)S(1)} %copy.72), channel_id=1, replica_groups=mesh['row'=8,'col'=4] {'row'}, dimensions={1} | all-to-all | bytes 2097152 | tf_op jit(solution)/shard_map/all_to_all | solution.py:74
  856.7 34.1 %reduce-scatter.21.cloned.1.call-done = bf16[128,1024]{1,0:T(8,128)(2,1)} async-done(((bf16[1024,1024]{1,0:T(8,128)(2,1)}), bf16[128,1024]{1,0:T(8,128)(2,1)}) %reduce-scatter.21.cloned.1.call-update) | async-done | bytes 262160 | tf_op jit(solution)/shard_map/reduce_scatter | solution.py:75
  935.1 31.0 %all_to_all.159 = bf16[128,8,512]{2,0,1:T(8,128)(2,1)S(1)} all-to-all(bf16[128,8,512]{2,0,1:T(8,128)(2,1)S(1)} %copy.73), channel_id=1, replica_groups=mesh['row'=8,'col'=4] {'row'}, dimensions={1} | all-to-all | bytes 2097152 | tf_op jit(solution)/shard_map/all_to_all | solution.py:74
  970.0 34.2 %reduce-scatter.23.cloned.1.call-done = bf16[128,1024]{1,0:T(8,128)(2,1)} async-done(((bf16[1024,1024]{1,0:T(8,128)(2,1)}), bf16[128,1024]{1,0:T(8,128)(2,1)}) %reduce-scatter.23.cloned.1.call-update) | async-done | bytes 262160 | tf_op jit(solution)/shard_map/reduce_scatter | solution.py:75
  (154 shorter events, 250.0 us)
Async XLA Ops:
  6.5 31.9 %all-gather.18.cloned.1.call-start = ((), (), s32[]{:S(2)}) async-start(), calls=%async_computation.27 | async-start | bytes 1310720 | tf_op jit(solution)/shard_map/all_gather | solution.py:34
  8.5 99.7 %reduce-scatter.9.cloned.1.call-start = ((), (), s32[]{:S(2)}) async-start(), calls=%async_computation.16 | async-start | bytes 2359296 | tf_op jit(solution)/shard_map/reduce_scatter | solution.py:36
  74.0 77.5 %all-reduce.7.cloned.1.call-start = ((), (), s32[]{:S(2)}) async-start(), calls=%async_computation.17 | async-start | bytes 131072 | tf_op jit(solution)/shard_map/psum | solution.py:56
  76.1 34.2 %copy-start.4 = (bf16[6,1024,128]{2,1,0:T(8,128)(2,1)S(1)}, bf16[6,1024,128]{2,1,0:T(8,128)(2,1)}, u32[]{:S(2)}) copy-start(bf16[6,1024,128]{2,1,0:T(8,128)(2,1)} %param.46) | copy-start | bytes 4718596
  110.2 70.6 %all-gather.20.cloned.1.call-start = ((), (), s32[]{:S(2)}) async-start(), calls=%async_computation.28 | async-start | bytes 1310720 | tf_op jit(solution)/shard_map/all_gather | solution.py:34
  154.2 97.6 %reduce-scatter.11.cloned.1.call-start = ((), (), s32[]{:S(2)}) async-start(), calls=%async_computation.18 | async-start | bytes 2359296 | tf_op jit(solution)/shard_map/reduce_scatter | solution.py:36
  217.6 77.3 %all-reduce.13.cloned.1.call-start = ((), (), s32[]{:S(2)}) async-start(), calls=%async_computation.35 | async-start | bytes 131072 | tf_op jit(solution)/shard_map/psum | solution.py:56
  253.7 69.8 %all-gather.22.cloned.1.call-start = ((), (), s32[]{:S(2)}) async-start(), calls=%async_computation.29 | async-start | bytes 1310720 | tf_op jit(solution)/shard_map/all_gather | solution.py:34
  296.9 97.6 %reduce-scatter.13.cloned.1.call-start = ((), (), s32[]{:S(2)}) async-start(), calls=%async_computation.19 | async-start | bytes 2359296 | tf_op jit(solution)/shard_map/reduce_scatter | solution.py:36
  360.3 76.7 %all-gather.24.cloned.1.call-start = ((), (), s32[]{:S(2)}) async-start(), calls=%async_computation.30 | async-start | bytes 1310720 | tf_op jit(solution)/shard_map/all_gather | solution.py:34
  413.9 94.0 %reduce-scatter.15.cloned.1.call-start = ((), (), s32[]{:S(2)}) async-start(), calls=%async_computation.20 | async-start | bytes 2359296 | tf_op jit(solution)/shard_map/reduce_scatter | solution.py:36
  473.8 61.0 %all-gather.16.cloned.1.call-start = ((), (), s32[]{:S(2)}) async-start(), calls=%async_computation.21 | async-start | bytes 1310720 | tf_op jit(solution)/shard_map/all_gather | solution.py:73
  508.0 97.2 %reduce-scatter.17.cloned.1.call-start = ((), (), s32[]{:S(2)}) async-start(), calls=%async_computation.22 | async-start | bytes 2359296 | tf_op jit(solution)/shard_map/reduce_scatter | solution.py:75
  571.0 77.4 %all-reduce.9.cloned.1.call-start = ((), (), s32[]{:S(2)}) async-start(), calls=%async_computation.23 | async-start | bytes 131072 | tf_op jit(solution)/shard_map/psum | solution.py:94
  573.1 75.3 %copy-start.9 = (bf16[128,1024]{1,0:T(8,128)(2,1)S(1)}, bf16[128,1024]{1,0:T(8,128)(2,1)}, u32[]{:S(2)}) copy-start(bf16[128,1024]{1,0:T(8,128)(2,1)} %reduce-scatter.11.cloned.1.call-done) | copy-start | bytes 786436
  573.1 75.3 %copy-start.10 = (bf16[128,1024]{1,0:T(8,128)(2,1)S(1)}, bf16[128,1024]{1,0:T(8,128)(2,1)}, u32[]{:S(2)}) copy-start(bf16[128,1024]{1,0:T(8,128)(2,1)} %reduce-scatter.13.cloned.1.call-done) | copy-start | bytes 786436
  573.1 75.3 %copy-start.11 = (bf16[128,1024]{1,0:T(8,128)(2,1)S(1)}, bf16[128,1024]{1,0:T(8,128)(2,1)}, u32[]{:S(2)}) copy-start(bf16[128,1024]{1,0:T(8,128)(2,1)} %reduce-scatter.9.cloned.1.call-done) | copy-start | bytes 786436
  607.2 70.0 %all-gather.26.cloned.1.call-start = ((), (), s32[]{:S(2)}) async-start(), calls=%async_computation.31 | async-start | bytes 1310720 | tf_op jit(solution)/shard_map/all_gather | solution.py:73
  650.5 97.6 %reduce-scatter.19.cloned.1.call-start = ((), (), s32[]{:S(2)}) async-start(), calls=%async_computation.24 | async-start | bytes 2359296 | tf_op jit(solution)/shard_map/reduce_scatter | solution.py:75
  713.9 77.3 %all-reduce.11.cloned.1.call-start = ((), (), s32[]{:S(2)}) async-start(), calls=%async_computation.34 | async-start | bytes 131072 | tf_op jit(solution)/shard_map/psum | solution.py:92
  750.1 69.8 %all-gather.28.cloned.1.call-start = ((), (), s32[]{:S(2)}) async-start(), calls=%async_computation.32 | async-start | bytes 1310720 | tf_op jit(solution)/shard_map/all_gather | solution.py:73
  793.2 97.6 %reduce-scatter.21.cloned.1.call-start = ((), (), s32[]{:S(2)}) async-start(), calls=%async_computation.25 | async-start | bytes 2359296 | tf_op jit(solution)/shard_map/reduce_scatter | solution.py:75
  856.6 76.6 %all-gather.30.cloned.1.call-start = ((), (), s32[]{:S(2)}) async-start(), calls=%async_computation.33 | async-start | bytes 1310720 | tf_op jit(solution)/shard_map/all_gather | solution.py:73
  910.1 94.0 %reduce-scatter.23.cloned.1.call-start = ((), (), s32[]{:S(2)}) async-start(), calls=%async_computation.26 | async-start | bytes 2359296 | tf_op jit(solution)/shard_map/reduce_scatter | solution.py:75
  (12 other events, 146.6 us)
Sparse Core Ops, SparseCore 0:
  9.2 29.2 all-gather.17
  74.1 34.0 reduce-scatter.8
  111.1 40.3 all-reduce.6
  154.3 26.4 all-gather.19
  217.7 34.0 reduce-scatter.10
  254.5 40.4 all-reduce.12
  297.0 26.4 all-gather.21
  360.4 34.0 reduce-scatter.12
  414.1 22.9 all-gather.23
  473.9 34.0 reduce-scatter.14
  509.8 24.9 all-gather.15
  571.1 34.0 reduce-scatter.16
  608.0 40.3 all-reduce.8
  650.7 26.4 all-gather.25
  714.1 34.0 reduce-scatter.18
  750.8 40.3 all-reduce.10
  793.3 26.4 all-gather.27
  856.8 34.0 reduce-scatter.20
  910.3 22.8 all-gather.29
  970.1 34.0 reduce-scatter.22
where the time goes:
time: 1020 us; the launch traced here: 1010 us
  waiting for transfers between devices  596 us (58%)
  blocking collectives  313 us (31%)
  matrix products  47.9 us (5%)
  local copies, waits for them, and re-layouts  38.9 us (4%)
  between operations  14.7 us (1%)
    all_to_all x8, blocking collectives, shards(): lax.all_to_all(whole, 'row', split_axis=1, concat_axis=0, tiled=True)  248 us
    all_gather x8, waiting for transfers between devices, shards(): whole = lax.all_gather(rounded, 'col', axis=1, tiled=True)  209 us
    reduce_scatter x4, waiting for transfers between devices, shards(): lax.psum_scatter(sum_terms(moved, inv_upper[section]).astype(jnp.bfloat16...  130 us
    reduce_scatter x4, waiting for transfers between devices, shards(): lax.psum_scatter(sum_terms(moved, inv_lower[section]).astype(jnp.bfloat16...  129 us
    psum x2, waiting for transfers between devices, shards(): lax.psum(projections[1:].astype(jnp.bfloat16), 'col').astype(jnp.float32)  63.3 us
    psum x1, waiting for transfers between devices, shards(): lax.psum(projections[-1:].astype(jnp.bfloat16), 'col').astype(jnp.float32)  39 us
    psum x2, blocking collectives, shards(): lax.psum(projections[-1:].astype(jnp.bfloat16), 'col').astype(jnp.float32)  32.5 us
    psum x2, blocking collectives, shards(): lax.psum(projections[:1].astype(jnp.bfloat16), 'col').astype(jnp.float32)  32.4 us
  transfers between devices with their start and end apart: 20, of which 20 were waited for; matrix products, arithmetic and copies ran while one was open for 1% of the time, Pallas kernels for 0%

commit v1 on v0

--- a/solution.py
+++ b/solution.py
@@ -89,7 +89,9 @@
                 up_right[pair_index],
                 preferred_element_type=jnp.float32,
             )
-            leading = lax.psum(projections[-1:].astype(jnp.bfloat16), "col").astype(jnp.float32)
+            leading = jnp.sum(
+                lax.all_gather(projections[-1:].astype(jnp.bfloat16), "col"), axis=0
+            ).astype(jnp.float32)
             if section > 1:
                 remaining = lax.psum(projections[:-1].astype(jnp.bfloat16), "col").astype(
                     jnp.float32

time: 1020 us -> 987 us (0.968)
  waiting for transfers between devices: 596 us -> 560 us
    psum x1 -> x0, waiting for transfers between devices: 39 us -> none  [shards(): lax.psum(projections[-1:].astype(jnp.bfloat16), 'col').astype(jnp.float32)]
    all_gather x0 -> x3, blocking collectives: none -> 25.6 us  [shards(): lax.all_gather(projections[-1:].astype(jnp.bfloat16), 'col')]
    psum x2 -> x1, blocking collectives: 32.5 us -> 15.3 us  [shards(): lax.psum(projections[:-1].astype(jnp.bfloat16), 'col').astype(jnp.float32)]
  transfers between devices with their start and end apart: 20 -> 19, of which waited for: 20 -> 19; matrix products, arithmetic and copies ran while one was open for 1% -> 2% of each run, Pallas kernels for 0% -> 0%
where the time goes in v1:
time: 987 us; the launch traced here: 985 us
  waiting for transfers between devices  560 us (57%)
  blocking collectives  321 us (33%)
  matrix products  47.2 us (5%)
  local copies, waits for them, and re-layouts  38.8 us (4%)
  between operations  14.4 us (1%)
    all_to_all x8, blocking collectives, shards(): lax.all_to_all(whole, 'row', split_axis=1, concat_axis=0, tiled=True)  248 us
    all_gather x8, waiting for transfers between devices, shards(): whole = lax.all_gather(rounded, 'col', axis=1, tiled=True)  207 us
    reduce_scatter x4, waiting for transfers between devices, shards(): lax.psum_scatter(sum_terms(moved, inv_lower[section]).astype(jnp.bfloat16...  129 us
    reduce_scatter x4, waiting for transfers between devices, shards(): lax.psum_scatter(sum_terms(moved, inv_upper[section]).astype(jnp.bfloat16...  128 us
    psum x2, waiting for transfers between devices, shards(): lax.psum(projections[1:].astype(jnp.bfloat16), 'col').astype(jnp.float32)  63.3 us
    psum x2, blocking collectives, shards(): lax.psum(projections[:1].astype(jnp.bfloat16), 'col').astype(jnp.float32)  32.4 us
    psum x1, waiting for transfers between devices, shards(): lax.psum(projections[:-1].astype(jnp.bfloat16), 'col').astype(jnp.float32)  31.6 us
    dot_general x8, matrix products, times_inverse(): lax.dot_general(block, inverse, (((1,), (1,)), ((), ())), preferred_eleme...  30.6 us
  transfers between devices with their start and end apart: 19, of which 19 were waited for; matrix products, arithmetic and copies ran while one was open for 2% of the time, Pallas kernels for 0%

profile of v1, /device:TPU:0, one launch (start us, length us, event | category | flops | bytes accessed | tf_op | source)
XLA Modules:
  0.0 985.0 jit_solution(2384068761201279928)
XLA Ops:
  8.5 29.9 %all-gather.21.cloned.1.call-done = bf16[1,128,4096]{1,2,0:T(8,128)(2,1)} async-done(((bf16[1,128,1024]{1,2,0:T(8,128)(2,1)}), bf16[1,128,4096]{1,2,0:T(8,128)(2,1)}) %all-gather.21.cloned.1.call-update) | async-done | bytes 1048592 | tf_op jit(solution)/shard_map/all_gather | solution.py:34
  38.4 31.2 %all_to_all.152 = bf16[128,8,512]{0,2,1:T(8,128)(2,1)S(1)} all-to-all(bf16[128,8,512]{0,2,1:T(8,128)(2,1)} %bitcast.170), channel_id=1, replica_groups=mesh['row'=8,'col'=4] {'row'}, dimensions={1} | all-to-all | bytes 2097152 | tf_op jit(solution)/shard_map/all_to_all | solution.py:35
  76.8 31.4 %reduce-scatter.9.cloned.1.call-done = bf16[128,1024]{1,0:T(8,128)(2,1)} async-done(((bf16[1024,1024]{1,0:T(8,128)(2,1)}), bf16[128,1024]{1,0:T(8,128)(2,1)}) %reduce-scatter.9.cloned.1.call-update) | async-done | bytes 262160 | tf_op jit(solution)/shard_map/reduce_scatter | solution.py:36
  127.2 24.3 %all-reduce.5.cloned.1.call-done = bf16[2,128,128]{1,2,0:T(8,128)(2,1)} async-done(((bf16[2,128,128]{1,2,0:T(8,128)(2,1)}), bf16[2,128,128]{1,2,0:T(8,128)(2,1)}) %all-reduce.5.cloned.1.call-update) | async-done | bytes 65552 | tf_op jit(solution)/shard_map/psum | solution.py:56
  154.2 26.6 %all-gather.23.cloned.1.call-done = bf16[1,128,4096]{2,1,0:T(8,128)(2,1)} async-done(((bf16[1,128,1024]{2,1,0:T(8,128)(2,1)}), bf16[1,128,4096]{2,1,0:T(8,128)(2,1)}) %all-gather.23.cloned.1.call-update) | async-done | bytes 1048592 | tf_op jit(solution)/shard_map/all_gather | solution.py:34
  182.8 31.0 %all_to_all.153 = bf16[128,8,512]{2,0,1:T(8,128)(2,1)S(1)} all-to-all(bf16[128,8,512]{2,0,1:T(8,128)(2,1)S(1)} %copy.97), channel_id=1, replica_groups=mesh['row'=8,'col'=4] {'row'}, dimensions={1} | all-to-all | bytes 2097152 | tf_op jit(solution)/shard_map/all_to_all | solution.py:35
  220.9 30.8 %reduce-scatter.11.cloned.1.call-done = bf16[128,1024]{1,0:T(8,128)(2,1)} async-done(((bf16[1024,1024]{1,0:T(8,128)(2,1)}), bf16[128,1024]{1,0:T(8,128)(2,1)}) %reduce-scatter.11.cloned.1.call-update) | async-done | bytes 262160 | tf_op jit(solution)/shard_map/reduce_scatter | solution.py:36
  255.9 39.0 %all-reduce.9.cloned.1.call-done = (bf16[1,128,128]{1,2,0:T(8,128)(2,1)}, bf16[1,128,128]{1,2,0:T(8,128)(2,1)}) async-done(((bf16[1,128,128]{1,2,0:T(8,128)(2,1)}, bf16[1,128,128]{1,2,0:T(8,128)(2,1)}), (bf16[1,128,128]{1,2,0:T(8,128)(2,1)}, bf16[1,128,128]{1,2,0:T(8,128)(2,1)})) %all-reduce.9.cloned.1.call-update) | async-done | bytes 65552 | tf_op jit(solution)/shard_map/psum | solution.py:56
  297.0 26.6 %all-gather.25.cloned.1.call-done = bf16[1,128,4096]{2,1,0:T(8,128)(2,1)} async-done(((bf16[1,128,1024]{2,1,0:T(8,128)(2,1)}), bf16[1,128,4096]{2,1,0:T(8,128)(2,1)}) %all-gather.25.cloned.1.call-update) | async-done | bytes 1048592 | tf_op jit(solution)/shard_map/all_gather | solution.py:34
  325.5 31.0 %all_to_all.154 = bf16[128,8,512]{2,0,1:T(8,128)(2,1)S(1)} all-to-all(bf16[128,8,512]{2,0,1:T(8,128)(2,1)S(1)} %copy.100), channel_id=1, replica_groups=mesh['row'=8,'col'=4] {'row'}, dimensions={1} | all-to-all | bytes 2097152 | tf_op jit(solution)/shard_map/all_to_all | solution.py:35
  361.7 32.8 %reduce-scatter.13.cloned.1.call-done = bf16[128,1024]{1,0:T(8,128)(2,1)} async-done(((bf16[1024,1024]{1,0:T(8,128)(2,1)}), bf16[128,1024]{1,0:T(8,128)(2,1)}) %reduce-scatter.13.cloned.1.call-update) | async-done | bytes 262160 | tf_op jit(solution)/shard_map/reduce_scatter | solution.py:36
  438.9 31.0 %all_to_all.155 = bf16[128,8,512]{2,0,1:T(8,128)(2,1)S(1)} all-to-all(bf16[128,8,512]{2,0,1:T(8,128)(2,1)S(1)} %copy.101), channel_id=1, replica_groups=mesh['row'=8,'col'=4] {'row'}, dimensions={1} | all-to-all | bytes 2097152 | tf_op jit(solution)/shard_map/all_to_all | solution.py:35
  473.8 34.1 %reduce-scatter.15.cloned.1.call-done = bf16[128,1024]{1,0:T(8,128)(2,1)} async-done(((bf16[1024,1024]{1,0:T(8,128)(2,1)}), bf16[128,1024]{1,0:T(8,128)(2,1)}) %reduce-scatter.15.cloned.1.call-update) | async-done | bytes 262160 | tf_op jit(solution)/shard_map/reduce_scatter | solution.py:36
  508.0 26.8 %all-gather.19.cloned.1.call-done = bf16[128,4096]{1,0:T(8,128)(2,1)} async-done(((bf16[128,1024]{1,0:T(8,128)(2,1)}), bf16[128,4096]{1,0:T(8,128)(2,1)}) %all-gather.19.cloned.1.call-update) | async-done | bytes 1048592 | tf_op jit(solution)/shard_map/all_gather | solution.py:73
  536.1 31.0 %all_to_all.156 = bf16[128,8,512]{2,0,1:T(8,128)(2,1)S(1)} all-to-all(bf16[128,8,512]{2,0,1:T(8,128)(2,1)S(1)} %bitcast.164), channel_id=1, replica_groups=mesh['row'=8,'col'=4] {'row'}, dimensions={1} | all-to-all | bytes 2097152 | tf_op jit(solution)/shard_map/all_to_all | solution.py:74
  573.8 31.4 %reduce-scatter.17.cloned.1.call-done = bf16[128,1024]{1,0:T(8,128)(2,1)} async-done(((bf16[1024,1024]{1,0:T(8,128)(2,1)}), bf16[128,1024]{1,0:T(8,128)(2,1)}) %reduce-scatter.17.cloned.1.call-update) | async-done | bytes 262160 | tf_op jit(solution)/shard_map/reduce_scatter | solution.py:75
  616.8 31.6 %all-reduce.7.cloned.1.call-done = bf16[2,128,128]{1,2,0:T(8,128)(2,1)} async-done(((bf16[2,128,128]{1,2,0:T(8,128)(2,1)}), bf16[2,128,128]{1,2,0:T(8,128)(2,1)}) %all-reduce.7.cloned.1.call-update) | async-done | bytes 65552 | tf_op jit(solution)/shard_map/psum | solution.py:96
  650.6 26.6 %all-gather.29.cloned.1.call-done = bf16[1,128,4096]{2,1,0:T(8,128)(2,1)} async-done(((bf16[1,128,1024]{2,1,0:T(8,128)(2,1)}), bf16[1,128,4096]{2,1,0:T(8,128)(2,1)}) %all-gather.29.cloned.1.call-update) | async-done | bytes 1048592 | tf_op jit(solution)/shard_map/all_gather | solution.py:73
  679.1 31.0 %all_to_all.157 = bf16[128,8,512]{2,0,1:T(8,128)(2,1)S(1)} all-to-all(bf16[128,8,512]{2,0,1:T(8,128)(2,1)S(1)} %copy.107), channel_id=1, replica_groups=mesh['row'=8,'col'=4] {'row'}, dimensions={1} | all-to-all | bytes 2097152 | tf_op jit(solution)/shard_map/all_to_all | solution.py:74
  719.5 28.8 %reduce-scatter.19.cloned.1.call-done = bf16[128,1024]{1,0:T(8,128)(2,1)} async-done(((bf16[1024,1024]{1,0:T(8,128)(2,1)}), bf16[128,1024]{1,0:T(8,128)(2,1)}) %reduce-scatter.19.cloned.1.call-update) | async-done | bytes 262160 | tf_op jit(solution)/shard_map/reduce_scatter | solution.py:75
  800.4 31.0 %all_to_all.158 = bf16[128,8,512]{2,0,1:T(8,128)(2,1)S(1)} all-to-all(bf16[128,8,512]{2,0,1:T(8,128)(2,1)S(1)} %copy.112), channel_id=1, replica_groups=mesh['row'=8,'col'=4] {'row'}, dimensions={1} | all-to-all | bytes 2097152 | tf_op jit(solution)/shard_map/all_to_all | solution.py:74
  835.3 34.1 %reduce-scatter.21.cloned.1.call-done = bf16[128,1024]{1,0:T(8,128)(2,1)} async-done(((bf16[1024,1024]{1,0:T(8,128)(2,1)}), bf16[128,1024]{1,0:T(8,128)(2,1)}) %reduce-scatter.21.cloned.1.call-update) | async-done | bytes 262160 | tf_op jit(solution)/shard_map/reduce_scatter | solution.py:75
  907.0 31.0 %all_to_all.159 = bf16[128,8,512]{2,0,1:T(8,128)(2,1)S(1)} all-to-all(bf16[128,8,512]{2,0,1:T(8,128)(2,1)S(1)} %copy.113), channel_id=1, replica_groups=mesh['row'=8,'col'=4] {'row'}, dimensions={1} | all-to-all | bytes 2097152 | tf_op jit(solution)/shard_map/all_to_all | solution.py:74
  941.8 34.2 %reduce-scatter.23.cloned.1.call-done = bf16[128,1024]{1,0:T(8,128)(2,1)} async-done(((bf16[1024,1024]{1,0:T(8,128)(2,1)}), bf16[128,1024]{1,0:T(8,128)(2,1)}) %reduce-scatter.23.cloned.1.call-update) | async-done | bytes 262160 | tf_op jit(solution)/shard_map/reduce_scatter | solution.py:75
  (160 shorter events, 233.6 us)
Async XLA Ops:
  6.5 31.9 %all-gather.21.cloned.1.call-start = ((), (), s32[]{:S(2)}) async-start(), calls=%async_computation.27 | async-start | bytes 1310720 | tf_op jit(solution)/shard_map/all_gather | solution.py:34
  8.5 99.7 %reduce-scatter.9.cloned.1.call-start = ((), (), s32[]{:S(2)}) async-start(), calls=%async_computation.16 | async-start | bytes 2359296 | tf_op jit(solution)/shard_map/reduce_scatter | solution.py:36
  74.0 77.5 %all-reduce.5.cloned.1.call-start = ((), (), s32[]{:S(2)}) async-start(), calls=%async_computation.17 | async-start | bytes 131072 | tf_op jit(solution)/shard_map/psum | solution.py:56
  76.1 34.2 %copy-start.4 = (bf16[6,1024,128]{2,1,0:T(8,128)(2,1)S(1)}, bf16[6,1024,128]{2,1,0:T(8,128)(2,1)}, u32[]{:S(2)}) copy-start(bf16[6,1024,128]{2,1,0:T(8,128)(2,1)} %param.46) | copy-start | bytes 4718596
  110.2 70.6 %all-gather.23.cloned.1.call-start = ((), (), s32[]{:S(2)}) async-start(), calls=%async_computation.28 | async-start | bytes 1310720 | tf_op jit(solution)/shard_map/all_gather | solution.py:34
  154.2 97.6 %reduce-scatter.11.cloned.1.call-start = ((), (), s32[]{:S(2)}) async-start(), calls=%async_computation.18 | async-start | bytes 2359296 | tf_op jit(solution)/shard_map/reduce_scatter | solution.py:36
  217.6 77.3 %all-reduce.9.cloned.1.call-start = ((), (), s32[]{:S(2)}) async-start(), calls=%async_computation.34 | async-start | bytes 131072 | tf_op jit(solution)/shard_map/psum | solution.py:56
  253.7 69.8 %all-gather.25.cloned.1.call-start = ((), (), s32[]{:S(2)}) async-start(), calls=%async_computation.29 | async-start | bytes 1310720 | tf_op jit(solution)/shard_map/all_gather | solution.py:34
  296.9 97.6 %reduce-scatter.13.cloned.1.call-start = ((), (), s32[]{:S(2)}) async-start(), calls=%async_computation.19 | async-start | bytes 2359296 | tf_op jit(solution)/shard_map/reduce_scatter | solution.py:36
  360.3 76.7 %all-gather.27.cloned.1.call-start = ((), (), s32[]{:S(2)}) async-start(), calls=%async_computation.30 | async-start | bytes 1310720 | tf_op jit(solution)/shard_map/all_gather | solution.py:34
  413.9 94.0 %reduce-scatter.15.cloned.1.call-start = ((), (), s32[]{:S(2)}) async-start(), calls=%async_computation.20 | async-start | bytes 2359296 | tf_op jit(solution)/shard_map/reduce_scatter | solution.py:36
  473.8 61.0 %all-gather.19.cloned.1.call-start = ((), (), s32[]{:S(2)}) async-start(), calls=%async_computation.21 | async-start | bytes 1310720 | tf_op jit(solution)/shard_map/all_gather | solution.py:73
  508.0 97.2 %reduce-scatter.17.cloned.1.call-start = ((), (), s32[]{:S(2)}) async-start(), calls=%async_computation.22 | async-start | bytes 2359296 | tf_op jit(solution)/shard_map/reduce_scatter | solution.py:75
  571.0 77.4 %all-reduce.7.cloned.1.call-start = ((), (), s32[]{:S(2)}) async-start(), calls=%async_computation.23 | async-start | bytes 131072 | tf_op jit(solution)/shard_map/psum | solution.py:96
  573.1 34.2 %copy-start.5 = (bf16[6,1024,128]{2,1,0:T(8,128)(2,1)S(1)}, bf16[6,1024,128]{2,1,0:T(8,128)(2,1)}, u32[]{:S(2)}) copy-start(bf16[6,1024,128]{2,1,0:T(8,128)(2,1)} %param.48) | copy-start | bytes 4718596
  573.1 75.3 %copy-start.9 = (bf16[128,1024]{1,0:T(8,128)(2,1)S(1)}, bf16[128,1024]{1,0:T(8,128)(2,1)}, u32[]{:S(2)}) copy-start(bf16[128,1024]{1,0:T(8,128)(2,1)} %reduce-scatter.11.cloned.1.call-done) | copy-start | bytes 786436
  573.1 75.3 %copy-start.10 = (bf16[128,1024]{1,0:T(8,128)(2,1)S(1)}, bf16[128,1024]{1,0:T(8,128)(2,1)}, u32[]{:S(2)}) copy-start(bf16[128,1024]{1,0:T(8,128)(2,1)} %reduce-scatter.13.cloned.1.call-done) | copy-start | bytes 786436
  573.1 75.3 %copy-start.11 = (bf16[128,1024]{1,0:T(8,128)(2,1)S(1)}, bf16[128,1024]{1,0:T(8,128)(2,1)}, u32[]{:S(2)}) copy-start(bf16[128,1024]{1,0:T(8,128)(2,1)} %reduce-scatter.9.cloned.1.call-done) | copy-start | bytes 786436
  607.2 70.0 %all-gather.29.cloned.1.call-start = ((), (), s32[]{:S(2)}) async-start(), calls=%async_computation.31 | async-start | bytes 1310720 | tf_op jit(solution)/shard_map/all_gather | solution.py:73
  650.5 97.7 %reduce-scatter.19.cloned.1.call-start = ((), (), s32[]{:S(2)}) async-start(), calls=%async_computation.24 | async-start | bytes 2359296 | tf_op jit(solution)/shard_map/reduce_scatter | solution.py:75
  713.9 84.5 %all-gather.31.cloned.1.call-start = ((), (), s32[]{:S(2)}) async-start(), calls=%async_computation.32 | async-start | bytes 1310720 | tf_op jit(solution)/shard_map/all_gather | solution.py:73
  775.0 94.5 %reduce-scatter.21.cloned.1.call-start = ((), (), s32[]{:S(2)}) async-start(), calls=%async_computation.25 | async-start | bytes 2359296 | tf_op jit(solution)/shard_map/reduce_scatter | solution.py:75
  835.3 69.8 %all-gather.33.cloned.1.call-start = ((), (), s32[]{:S(2)}) async-start(), calls=%async_computation.33 | async-start | bytes 1310720 | tf_op jit(solution)/shard_map/all_gather | solution.py:73
  881.1 94.9 %reduce-scatter.23.cloned.1.call-start = ((), (), s32[]{:S(2)}) async-start(), calls=%async_computation.26 | async-start | bytes 2359296 | tf_op jit(solution)/shard_map/reduce_scatter | solution.py:75
  (11 other events, 112.3 us)
Sparse Core Ops, SparseCore 0:
  9.2 29.2 all-gather.20
  74.1 34.0 reduce-scatter.8
  111.1 40.3 all-reduce.4
  154.3 26.4 all-gather.22
  217.7 34.0 reduce-scatter.10
  254.5 40.4 all-reduce.8
  297.0 26.4 all-gather.24
  360.4 34.0 reduce-scatter.12
  414.1 22.9 all-gather.26
  473.9 34.0 reduce-scatter.14
  509.8 24.9 all-gather.18
  571.1 34.0 reduce-scatter.16
  608.0 40.3 all-reduce.6
  650.7 26.4 all-gather.28
  714.1 34.1 reduce-scatter.18
  775.1 23.3 all-gather.30
  835.4 34.0 reduce-scatter.20
  881.2 23.8 all-gather.32
  941.9 34.0 reduce-scatter.22
